TPU v7x, 32 devices: a whole 2x2x4 slice. The times are simulated.
32 devices in a mesh: grp: 2 (over y), tile: 4 (over z), coil: 2 (over x), spk: 2 (over core).
Axes of the slice: x: 2, y: 2, z: 4, core: 2. Of those that a mesh axis runs over, the one named last changes fastest.
Arguments:
- coil_maps: float32 [2, 512, 2, 256], P('coil', ('grp', 'tile', 'spk')), parts along dimension 1, may hold values from -6 to 6
- kspace_data: bfloat16 [2, 128, 2, 256], P('coil', ('grp', 'tile', 'spk')), parts along dimension 1, may hold values from -24 to 24
- interp_weights: bfloat16 [128, 6, 256], P(('grp', 'tile', 'spk')), parts along dimension 0, may hold values from 0.099609375 to 1
- sample_bins: int32 [128, 256], P(('grp', 'tile', 'spk')), parts along dimension 0, may hold values from 0 to 65535, as said below
- spoke_count: int32 [16], P(('grp', 'tile', 'spk')), parts along dimension 0, may hold values from 1 to 8, 32 in all
- thresholds: float32 [3], replicated, may hold values from 0.05 to 0.3
Outputs:
- image: float32 [512, 2, 256], P(('grp', 'tile', 'spk')), parts along dimension 0
There are 2 independent parts, one for each index of `grp`. A program takes and returns all parts, laid end to end along the dimension named above; an argument that names none is the same for every part. Nothing has to cross between parts.
Inputs may be any that keep to these rules, and one draw needn't show every extreme that they name: `sample_bins`: sample k of each spoke lies on a straight line through cell (128, 128), at offset k - 128 along the spoke's direction, coordinates taken modulo 256. `spoke_count`: each independent slice has its own 8 counts, and the whole array holds one such block of counts per slice. The 8 counts of each slice sum to 32. In every draw, at least one device of each slice holds 8 live spokes. A device's live spokes are its first ones.
All inputs are finite; a program needn't handle non-finite values.
Results may differ from a plain program's by a relative error of at most 0.0016.
Values may be sent and summed in bfloat16 or wider, within the bound.
A program may use at most 64 MiB of HBM per device.

v0:
```python
import math
import jax
import jax.numpy as jnp
from jax import lax
from jax.sharding import PartitionSpec as P

N = 256
RO = 256
SPK_DEV = 8
LEVELS = 3
ITERS = 4
HIGH = lax.Precision.HIGHEST
STEP_SIZE = 0.5
RSQRT2 = 0.7071067811865476


def dft_table(length, direction):
    positions = jnp.arange(length, dtype=jnp.int32)
    phases = positions[:, None] * positions[None, :] % length
    angles = phases.astype(jnp.float32) * jnp.float32(2.0 * math.pi / length)
    norm_scale = 1.0 / math.sqrt(length)
    cosine = jnp.cos(angles) * norm_scale
    sine_tab = jnp.sin(angles) * norm_scale
    top_rows = jnp.stack([cosine, -direction * sine_tab], axis=1)
    bottom = jnp.stack([direction * sine_tab, cosine], axis=1)
    return jnp.stack([top_rows, bottom], axis=0)


def haar_matrix(length, levels):
    haar_mat = jnp.eye(length, dtype=jnp.float32)
    positions = jnp.arange(length, dtype=jnp.int32)
    out_i = positions[:, None]
    in_j = positions[None, :]
    for level_num in range(levels):
        span_len = length >> level_num
        half_len = span_len // 2
        low_hit = (out_i < half_len) & ((in_j == 2 * out_i) | (in_j == 2 * out_i + 1))
        high_pos = out_i - half_len
        high_hit = (
            (out_i >= half_len)
            & (out_i < span_len)
            & ((in_j == 2 * high_pos) | (in_j == 2 * high_pos + 1))
        )
        sign_val = jnp.where(in_j == 2 * high_pos + 1, -1.0, 1.0)
        step_mat = jnp.where(low_hit, RSQRT2, jnp.where(high_hit, sign_val * RSQRT2, 0.0))
        step_mat = step_mat + jnp.where((out_i >= span_len) & (in_j == out_i), 1.0, 0.0)
        haar_mat = jnp.dot(step_mat.astype(jnp.float32), haar_mat, precision=HIGH)
    return haar_mat


def haar_labels(length, levels):
    positions = jnp.arange(length, dtype=jnp.int32)
    band_label = jnp.ones((length,), jnp.int32)
    for level_num in range(1, levels + 1):
        band_label = band_label + (positions < length >> level_num).astype(jnp.int32)
    return band_label


def wavelet_shrink(target, thresholds, levels):
    row_count, pair_dim, col_count = target.shape
    block_len = 2**levels
    row_haar = haar_matrix(block_len, levels)
    col_haar = haar_matrix(col_count, levels)
    grouped = target.reshape(row_count // block_len, block_len, pair_dim, col_count)
    coeffs = jnp.einsum("ij,gjpc->gipc", row_haar, grouped, precision=HIGH)
    coeffs = jnp.einsum("gipc,kc->gipk", coeffs, col_haar, precision=HIGH)
    band_min = jnp.minimum(
        haar_labels(block_len, levels)[:, None], haar_labels(col_count, levels)[None, :]
    )
    active = band_min <= levels
    limits = jnp.ones(band_min.shape, jnp.float32)
    for level_num in range(levels):
        limits = jnp.where(band_min == level_num + 1, thresholds[level_num], limits)
    magnitude = jnp.sqrt(coeffs[:, :, 0] ** 2 + coeffs[:, :, 1] ** 2)
    factor = jnp.maximum(magnitude - limits, 0.0) / jnp.maximum(magnitude, limits)
    factor = jnp.where(active, factor, 1.0)
    shrunk = coeffs * factor[:, :, None, :]
    restored = jnp.einsum("gipk,kc->gipc", shrunk, col_haar, precision=HIGH)
    restored = jnp.einsum("ij,gipc->gjpc", row_haar, restored, precision=HIGH)
    return restored.reshape(row_count, pair_dim, col_count)


def complex_mul(left, right):
    real_part = left[:, 0] * right[:, 0] - left[:, 1] * right[:, 1]
    imag_part = left[:, 0] * right[:, 1] + left[:, 1] * right[:, 0]
    return jnp.stack([real_part, imag_part], axis=1)


def conj_mul(left, right):
    real_part = left[:, 0] * right[:, 0] + left[:, 1] * right[:, 1]
    imag_part = left[:, 0] * right[:, 1] - left[:, 1] * right[:, 0]
    return jnp.stack([real_part, imag_part], axis=1)


def interp_tables(load_bins, load_interp):
    grid_ids = jnp.arange(N, dtype=jnp.int32)
    row_bins = load_bins // N
    col_bins = load_bins % N
    zero_val = jnp.zeros((), jnp.bfloat16)
    row_table = jnp.zeros((load_bins.shape[0], load_bins.shape[1], N), jnp.bfloat16)
    col_table = jnp.zeros((load_bins.shape[0], N, load_bins.shape[1]), jnp.bfloat16)
    for tap_index in range(3):
        row_hit = grid_ids[None, None, :] == ((row_bins + tap_index - 1) % N)[:, :, None]
        row_table = row_table + jnp.where(
            row_hit, load_interp[:, tap_index, :][:, :, None], zero_val
        )
        col_hit = grid_ids[None, :, None] == ((col_bins + tap_index - 1) % N)[:, None, :]
        col_table = col_table + jnp.where(
            col_hit, load_interp[:, 3 + tap_index, :][:, None, :], zero_val
        )
    return (row_table, col_table)


def local(coil_maps, kspace_data, interp_weights, sample_bins, spoke_count, thresholds):
    blocks = lax.axis_size(("tile", "spk"))
    row_count = coil_maps.shape[1]
    live_total = blocks * SPK_DEV // 2
    coil_sens = coil_maps[0]
    measured = kspace_data[0]
    my_index = lax.axis_index(("tile", "spk"))
    counts = lax.all_gather(spoke_count, ("tile", "spk"), axis=0, tiled=True)
    prefix = jnp.cumsum(counts) - counts
    per_peer = -(-SPK_DEV // blocks)
    peer_ids = jnp.arange(blocks, dtype=jnp.int32)
    first_slot = (peer_ids - prefix[my_index]) % blocks
    slot_index = first_slot[:, None] + blocks * jnp.arange(per_peer, dtype=jnp.int32)[None, :]
    picked = jnp.clip(slot_index, 0, SPK_DEV - 1)
    values = jnp.concatenate([measured, interp_weights], axis=1)
    got_values = lax.all_to_all(
        values[picked], ("tile", "spk"), split_axis=0, concat_axis=0, tiled=True
    )
    got_bins = lax.all_to_all(
        sample_bins[picked], ("tile", "spk"), split_axis=0, concat_axis=0, tiled=True
    )
    my_share = SPK_DEV // 2
    wanted = my_index + blocks * jnp.arange(my_share, dtype=jnp.int32)
    source = jnp.sum((prefix[None, :] <= wanted[:, None]).astype(jnp.int32), axis=1) - 1
    depth_at = (wanted - prefix[source]) // blocks
    loaded = got_values[source, depth_at]
    load_bins = got_bins[source, depth_at]
    load_data = loaded[:, 0:2]
    load_interp = loaded[:, 2:8]
    row_table, col_table = interp_tables(load_bins, load_interp)
    n_load = row_table.shape[0]
    offset = jnp.abs(jnp.arange(RO, dtype=jnp.int32) - RO // 2).astype(jnp.float32)
    density = (offset + 0.5) * (N / (3.0 * RO * live_total))
    target_data = load_data.astype(jnp.float32)
    fwd_table = dft_table(N, 1.0)
    inv_table = dft_table(N, -1.0)

    def grid_rows(weighted):

        def grid_term(row_start, piece_rows):

            def grid_one_spoke(spoke_index, partial_value):
                row_one = lax.dynamic_index_in_dim(row_table, spoke_index, 0, keepdims=False)
                col_one = lax.dynamic_index_in_dim(col_table, spoke_index, 0, keepdims=False)
                col_slice = col_one.astype(jnp.float32)
                residue = lax.dynamic_index_in_dim(weighted, spoke_index, 0, keepdims=False)
                smeared = (col_slice[:, None, :] * residue[None, :, :]).astype(jnp.bfloat16)
                added = jnp.dot(
                    smeared.reshape(piece_rows * 2, RO), row_one, preferred_element_type=jnp.float32
                )
                return partial_value + added.reshape(piece_rows, 2, N)

            return lax.fori_loop(
                0, my_share, grid_one_spoke, jnp.zeros((piece_rows, 2, N), jnp.float32)
            )

        return grid_term

    estimate = jnp.zeros((row_count, 2, N), jnp.float32)
    for iteration in range(ITERS):
        if iteration == 0:
            weighted = -density[None, None, :] * target_data
        else:
            coil_image = complex_mul(coil_sens, estimate)
            half_done = jnp.einsum("rpc,pcqv->rqv", coil_image, fwd_table, precision=HIGH)
            turned = lax.all_to_all(
                half_done, ("tile", "spk"), split_axis=2, concat_axis=0, tiled=True
            )
            kspace = jnp.einsum("rpv,prqu->vqu", turned, fwd_table, precision=HIGH).astype(
                jnp.bfloat16
            )
            piece = lax.all_gather(kspace, ("tile", "spk"), axis=0, tiled=True)
            fold_piece_rows = piece.shape[0]
            flat_piece = piece.reshape(fold_piece_rows * 2, N)

            def fold_one_spoke(spoke_index, partial_value):
                row_one = lax.dynamic_index_in_dim(row_table, spoke_index, 0, keepdims=False)
                col_one = lax.dynamic_index_in_dim(col_table, spoke_index, 0, keepdims=False)
                inner_sum = lax.dot_general(
                    flat_piece,
                    row_one,
                    (((1,), (1,)), ((), ())),
                    preferred_element_type=jnp.float32,
                )
                inner_sum = inner_sum.reshape(fold_piece_rows, 2, RO)
                col_slice = col_one.astype(jnp.float32)
                added = jnp.sum(inner_sum * col_slice[:, None, :], axis=0)
                current = lax.dynamic_index_in_dim(partial_value, spoke_index, 0, keepdims=False)
                return lax.dynamic_update_index_in_dim(
                    partial_value, current + added, spoke_index, 0
                )

            sample_model = lax.fori_loop(
                0, my_share, fold_one_spoke, jnp.zeros((n_load, 2, RO), jnp.float32)
            )
            weighted = density[None, None, :] * (sample_model - target_data)
        grid_term = grid_rows(weighted)
        owned_rows = lax.psum_scatter(
            grid_term(jnp.int32(0), row_count * lax.axis_size(("tile", "spk"))),
            ("tile", "spk"),
            scatter_dimension=0,
            tiled=True,
        )
        partial_back = jnp.einsum("vpu,puqr->vqr", owned_rows, inv_table, precision=HIGH)
        returned = lax.all_to_all(
            partial_back, ("tile", "spk"), split_axis=2, concat_axis=0, tiled=True
        )
        coil_back = jnp.einsum("vpr,pvqc->rqc", returned, inv_table, precision=HIGH)
        gradient = lax.psum(conj_mul(coil_sens, coil_back), "coil")
        estimate = wavelet_shrink(estimate - STEP_SIZE * gradient, thresholds, LEVELS)
    return estimate


def solution(mesh):
    placed = (
        P("coil", ("grp", "tile", "spk"), None, None),
        P("coil", ("grp", "tile", "spk"), None, None),
        P(("grp", "tile", "spk"), None, None),
        P(("grp", "tile", "spk"), None),
        P(("grp", "tile", "spk")),
        P(),
    )
    return jax.shard_map(
        local,
        mesh=mesh,
        in_specs=placed,
        out_specs=P(("grp", "tile", "spk"), None, None),
        check_vma=False,
    )
```

profile of v0, /device:TPU:0, one launch (start us, length us, event | category | flops | bytes accessed | tf_op | source)
XLA Modules:
  0.0 512.3 jit_solution(6684872715194408570)
XLA Ops:
  9.2 10.6 %all-reduce = s32[8]{0:T(128)S(1)} all-reduce(s32[8]{0:T(128)S(1)} %dynamic-update-slice), channel_id=1, replica_groups=mesh['grp'=2,'tile'=4,'coil'=2,'spk'=2] {'tile','spk'}, use_global_device_ids=true, to_apply=%add | all-reduce | flops 8 | bytes 64
  22.5 3.3 all-to-all-start
  34.2 5.0 all-to-all-start.1
  39.9 5.1 all-to-all-done.1
  47.7 7.5 %while.98 = (s32[]{:T(128)}, f32[256,2,256]{2,0,1:T(8,128)}, bf16[4,256,256]{2,1,0:T(8,128)(2,1)S(1)}, f32[4,2,256]{2,1,0:T(2,128)S(1)}, bf16[4,256,256]{2,1,0:T(8,128)(2,1)S(1)}, /*index=5*/s32[]{:T(128)}, s32[]{:T(128)}) while((s32[]{:T(128)}, f32[256,2,256]{2,0,1:T(8,128)}, bf16[4,256,256]{2,1,0:T(8,128)(2,1)S(1)}, ...), condition=%wide.region_3.4_spmd.clone, body=%wide.region_2.3_spmd.clone.sunk | while | flops 67698688 | bytes 1841251 | solution.py:166
  48.8 2.1 convolution_add_fusion.8
  51.0 2.1 convolution_add_fusion.8
  53.1 2.1 convolution_add_fusion.8
  57.0 2.7 select_select_fusion
  60.5 24.4 %reduce-scatter.5.cloned.1.call-done = f32[32,2,256]{2,0,1:T(8,128)} async-done(((f32[256,2,256]{2,0,1:T(8,128)}), f32[32,2,256]{2,0,1:T(8,128)}) %reduce-scatter.5.cloned.1.call-update) | async-done | bytes 65552 | tf_op jit(solution)/shard_map/reduce_scatter | solution.py:211
  89.2 3.4 all-to-all-start.2
  94.6 3.8 all-to-all-done.2
  107.4 18.6 %all-reduce.6.cloned.1.call-done = f32[32,2,256]{2,0,1:T(8,128)} async-done(((f32[32,2,256]{2,0,1:T(8,128)}), f32[32,2,256]{2,0,1:T(8,128)}) %all-reduce.6.cloned.1.call-update) | async-done | bytes 65552 | tf_op jit(solution)/shard_map/psum | solution.py:222
  133.2 4.6 all-to-all-start.3
  138.6 5.2 %all-to-all-done.3 = f32[8,1,2048]{2,1,0:T(1,128)} async-done(((f32[8,1,2048]{2,1,0:T(1,128)}), f32[8,1,2048]{2,1,0:T(1,128)}, u32[]{:S(2)}, u32[]{:S(2)}) %all-to-all-start.3) | async-done | bytes 65568 | tf_op jit(solution)/shard_map/all_to_all | solution.py:179
  143.8 2.2 reduce.1
  152.9 14.2 %all_gather.13 = bf16[256,2,256]{2,0,1:T(8,128)(2,1)S(1)} all-gather(bf16[32,2,256]{2,0,1:T(8,128)(2,1)S(1)} %fusion.32), channel_id=1, replica_groups=mesh['grp'=2,'tile'=4,'coil'=2,'spk'=2] {'tile','spk'}, dimensions={0}, use_global_device_ids=true | all-gather | bytes 294912 | tf_op jit(solution)/shard_map/all_gather | solution.py:185
  168.1 12.7 %while.95 = (s32[]{:T(128)}, f32[4,2,256]{2,1,0:T(2,128)}, bf16[4,256,256]{2,1,0:T(8,128)(2,1)S(1)}, bf16[512,256]{1,0:T(8,128)(2,1)S(1)}, bf16[4,256,256]{2,1,0:T(8,128)(2,1)S(1)}, /*index=5*/s32[]{:T(128)}) while((s32[]{:T(128)}, f32[4,2,256]{2,1,0:T(2,128)}, bf16[4,256,256]{2,1,0:T(8,128)(2,1)S(1)}, bf16[512,256]{1,0:T(8,128)(2,1)S(1)}, ...), condition=%wide.region_8.9_spmd, body=%wide.region_6.8_spmd.sunk | while | flops 67436544 | bytes 6300293 | solution.py:206
  182.3 7.5 %while.99 = (s32[]{:T(128)}, f32[256,2,256]{2,0,1:T(8,128)}, bf16[4,256,256]{2,1,0:T(8,128)(2,1)S(1)}, f32[4,2,256]{2,1,0:T(2,128)S(1)}, bf16[4,256,256]{2,1,0:T(8,128)(2,1)S(1)}, /*index=5*/s32[]{:T(128)}, s32[]{:T(128)}) while((s32[]{:T(128)}, f32[256,2,256]{2,0,1:T(8,128)}, bf16[4,256,256]{2,1,0:T(8,128)(2,1)S(1)}, ...), condition=%wide.region_10.11_spmd.clone, body=%wide.region_9.10_spmd.clone.sunk | while | flops 67698688 | bytes 1841251 | solution.py:166
  183.4 2.1 convolution_add_fusion.9
  185.5 2.1 convolution_add_fusion.9
  187.6 2.1 convolution_add_fusion.9
  189.8 28.9 %reduce-scatter.7.cloned.1.call-done = f32[32,2,256]{2,0,1:T(8,128)} async-done(((f32[256,2,256]{2,0,1:T(8,128)}), f32[32,2,256]{2,0,1:T(8,128)}) %reduce-scatter.7.cloned.1.call-update) | async-done | bytes 65552 | tf_op jit(solution)/shard_map/reduce_scatter | solution.py:211
  220.7 8.3 %all_to_all.136 = f32[8,1,2048]{2,1,0:T(1,128)S(1)} all-to-all(f32[8,1,2048]{2,1,0:T(1,128)S(1)} %reshape.884), channel_id=1, replica_groups=mesh['grp'=2,'tile'=4,'coil'=2,'spk'=2] {'tile','spk'}, dimensions={0} | all-to-all | bytes 131072 | tf_op jit(solution)/shard_map/all_to_all | solution.py:218
  231.7 19.7 %all-reduce.8.cloned.1.call-done = f32[32,2,256]{2,0,1:T(8,128)} async-done(((f32[32,2,256]{2,0,1:T(8,128)}), f32[32,2,256]{2,0,1:T(8,128)}) %all-reduce.8.cloned.1.call-update) | async-done | bytes 65552 | tf_op jit(solution)/shard_map/psum | solution.py:222
  258.9 4.6 all-to-all-start.5
  263.5 6.0 %all-to-all-done.5 = f32[8,1,2048]{2,1,0:T(1,128)} async-done(((f32[8,1,2048]{2,1,0:T(1,128)}), f32[8,1,2048]{2,1,0:T(1,128)}, u32[]{:S(2)}, u32[]{:S(2)}) %all-to-all-start.5) | async-done | bytes 65568 | tf_op jit(solution)/shard_map/all_to_all | solution.py:179
  269.5 2.2 reduce.3
  278.6 14.2 %all_gather.14 = bf16[256,2,256]{2,0,1:T(8,128)(2,1)S(1)} all-gather(bf16[32,2,256]{2,0,1:T(8,128)(2,1)S(1)} %fusion.33), channel_id=1, replica_groups=mesh['grp'=2,'tile'=4,'coil'=2,'spk'=2] {'tile','spk'}, dimensions={0}, use_global_device_ids=true | all-gather | bytes 294912 | tf_op jit(solution)/shard_map/all_gather | solution.py:185
  293.8 12.7 %while.96 = (s32[]{:T(128)}, f32[4,2,256]{2,1,0:T(2,128)}, bf16[4,256,256]{2,1,0:T(8,128)(2,1)S(1)}, bf16[512,256]{1,0:T(8,128)(2,1)S(1)}, bf16[4,256,256]{2,1,0:T(8,128)(2,1)S(1)}, /*index=5*/s32[]{:T(128)}) while((s32[]{:T(128)}, f32[4,2,256]{2,1,0:T(2,128)}, bf16[4,256,256]{2,1,0:T(8,128)(2,1)S(1)}, bf16[512,256]{1,0:T(8,128)(2,1)S(1)}, ...), condition=%wide.region_15.16_spmd, body=%wide.region_13.15_spmd.sunk | while | flops 67436544 | bytes 6300293 | solution.py:206
  307.9 7.5 %while.100 = (s32[]{:T(128)}, f32[256,2,256]{2,0,1:T(8,128)}, bf16[4,256,256]{2,1,0:T(8,128)(2,1)S(1)}, f32[4,2,256]{2,1,0:T(2,128)S(1)}, bf16[4,256,256]{2,1,0:T(8,128)(2,1)S(1)}, /*index=5*/s32[]{:T(128)}, s32[]{:T(128)}) while((s32[]{:T(128)}, f32[256,2,256]{2,0,1:T(8,128)}, bf16[4,256,256]{2,1,0:T(8,128)(2,1)S(1)}, ...), condition=%wide.region_17.18_spmd.clone, body=%wide.region_16.17_spmd.clone.sunk | while | flops 67698688 | bytes 1841251 | solution.py:166
  309.0 2.1 convolution_add_fusion.10
  311.1 2.1 convolution_add_fusion.10
  315.6 28.8 %reduce-scatter.9.cloned.1.call-done = f32[32,2,256]{2,0,1:T(8,128)} async-done(((f32[256,2,256]{2,0,1:T(8,128)}), f32[32,2,256]{2,0,1:T(8,128)}) %reduce-scatter.9.cloned.1.call-update) | async-done | bytes 65552 | tf_op jit(solution)/shard_map/reduce_scatter | solution.py:211
  346.4 8.3 %all_to_all.137 = f32[8,1,2048]{2,1,0:T(1,128)S(1)} all-to-all(f32[8,1,2048]{2,1,0:T(1,128)S(1)} %reshape.888), channel_id=1, replica_groups=mesh['grp'=2,'tile'=4,'coil'=2,'spk'=2] {'tile','spk'}, dimensions={0} | all-to-all | bytes 131072 | tf_op jit(solution)/shard_map/all_to_all | solution.py:218
  357.4 19.5 %all-reduce.10.cloned.1.call-done = f32[32,2,256]{2,0,1:T(8,128)} async-done(((f32[32,2,256]{2,0,1:T(8,128)}), f32[32,2,256]{2,0,1:T(8,128)}) %all-reduce.10.cloned.1.call-update) | async-done | bytes 65552 | tf_op jit(solution)/shard_map/psum | solution.py:222
  384.4 4.6 all-to-all-start.7
  389.0 6.0 %all-to-all-done.7 = f32[8,1,2048]{2,1,0:T(1,128)} async-done(((f32[8,1,2048]{2,1,0:T(1,128)}), f32[8,1,2048]{2,1,0:T(1,128)}, u32[]{:S(2)}, u32[]{:S(2)}) %all-to-all-start.7) | async-done | bytes 65568 | tf_op jit(solution)/shard_map/all_to_all | solution.py:179
  395.0 2.2 reduce.5
  404.1 14.2 %all_gather.15 = bf16[256,2,256]{2,0,1:T(8,128)(2,1)S(1)} all-gather(bf16[32,2,256]{2,0,1:T(8,128)(2,1)S(1)} %fusion.34), channel_id=1, replica_groups=mesh['grp'=2,'tile'=4,'coil'=2,'spk'=2] {'tile','spk'}, dimensions={0}, use_global_device_ids=true | all-gather | bytes 294912 | tf_op jit(solution)/shard_map/all_gather | solution.py:185
  419.3 12.7 %while.97 = (s32[]{:T(128)}, f32[4,2,256]{2,1,0:T(2,128)}, bf16[4,256,256]{2,1,0:T(8,128)(2,1)S(1)}, bf16[512,256]{1,0:T(8,128)(2,1)S(1)}, bf16[4,256,256]{2,1,0:T(8,128)(2,1)S(1)}, /*index=5*/s32[]{:T(128)}) while((s32[]{:T(128)}, f32[4,2,256]{2,1,0:T(2,128)}, bf16[4,256,256]{2,1,0:T(8,128)(2,1)S(1)}, bf16[512,256]{1,0:T(8,128)(2,1)S(1)}, ...), condition=%wide.region_22.23_spmd, body=%wide.region_20.22_spmd.sunk | while | flops 67436544 | bytes 6300293 | solution.py:206
  433.5 7.5 %while.101 = (s32[]{:T(128)}, f32[256,2,256]{2,0,1:T(8,128)}, bf16[4,256,256]{2,1,0:T(8,128)(2,1)S(1)}, f32[4,2,256]{2,1,0:T(2,128)S(1)}, bf16[4,256,256]{2,1,0:T(8,128)(2,1)S(1)}, /*index=5*/s32[]{:T(128)}, s32[]{:T(128)}) while((s32[]{:T(128)}, f32[256,2,256]{2,0,1:T(8,128)}, bf16[4,256,256]{2,1,0:T(8,128)(2,1)S(1)}, ...), condition=%wide.region_24.25_spmd.clone, body=%wide.region_23.24_spmd.clone.sunk | while | flops 67698688 | bytes 1841251 | solution.py:166
  434.6 2.1 convolution_add_fusion.11
  436.7 2.1 convolution_add_fusion.11
  438.9 2.1 convolution_add_fusion.11
  441.0 28.9 %reduce-scatter.11.cloned.1.call-done = f32[32,2,256]{2,0,1:T(8,128)} async-done(((f32[256,2,256]{2,0,1:T(8,128)}), f32[32,2,256]{2,0,1:T(8,128)}) %reduce-scatter.11.cloned.1.call-update) | async-done | bytes 65552 | tf_op jit(solution)/shard_map/reduce_scatter | solution.py:211
  472.0 8.3 %all_to_all.138 = f32[8,1,2048]{2,1,0:T(1,128)S(1)} all-to-all(f32[8,1,2048]{2,1,0:T(1,128)S(1)} %reshape.892), channel_id=1, replica_groups=mesh['grp'=2,'tile'=4,'coil'=2,'spk'=2] {'tile','spk'}, dimensions={0} | all-to-all | bytes 131072 | tf_op jit(solution)/shard_map/all_to_all | solution.py:218
  483.0 19.5 %all-reduce.12.cloned.1.call-done = f32[32,2,256]{2,0,1:T(8,128)} async-done(((f32[32,2,256]{2,0,1:T(8,128)}), f32[32,2,256]{2,0,1:T(8,128)}) %all-reduce.12.cloned.1.call-update) | async-done | bytes 65552 | tf_op jit(solution)/shard_map/psum | solution.py:222
  (406 shorter events, 145.9 us)
Async XLA Ops:
  6.5 14.8 %copy-start = (s32[8,256]{1,0:T(8,128)S(1)}, s32[8,256]{1,0:T(8,128)}, u32[]{:S(2)}) copy-start(s32[8,256]{1,0:T(8,128)} %param.23) | copy-start | bytes 24580
  22.5 11.7 %all-to-all-start = ((s32[8,1,256]{2,1,0:T(1,128)}), s32[8,1,256]{2,1,0:T(1,128)S(1)}, u32[]{:S(2)}, u32[]{:S(2)}) async-start(s32[8,1,256]{2,1,0:T(1,128)} %copy.115), calls=%async_computation | async-start | bytes 16384 | tf_op jit(solution)/shard_map/all_to_all | solution.py:132
  27.9 31.9 %copy-start.26 = (s32[8]{0:T(128)}, s32[8]{0:T(128)S(1)}, u32[]{:S(2)}) copy-start(s32[8]{0:T(128)S(1)} %get-tuple-element.881) | copy-start | bytes 100
  27.9 31.9 %copy-start.28 = (s32[8]{0:T(128)}, s32[8]{0:T(128)S(1)}, u32[]{:S(2)}) copy-start(s32[8]{0:T(128)S(1)} %get-tuple-element.882) | copy-start | bytes 100
  28.9 0.7 copy-start.19
  29.7 1.3 copy-start.23
  31.2 120.2 %copy-start.1 = (f32[1,256,2,256]{3,1,2,0:T(8,128)}, f32[1,256,2,256]{3,1,2,0:T(8,128)S(1)}, u32[]{:S(2)}) copy-start(f32[1,256,2,256]{3,1,2,0:T(8,128)S(1)} %get-tuple-element.830) | copy-start | bytes 1572868
  31.2 120.2 %copy-start.4 = (f32[1,256,2,256]{3,1,2,0:T(8,128)}, f32[1,256,2,256]{3,1,2,0:T(8,128)S(1)}, u32[]{:S(2)}) copy-start(f32[1,256,2,256]{3,1,2,0:T(8,128)S(1)} %get-tuple-element.833) | copy-start | bytes 1572868
  34.2 10.8 %all-to-all-start.1 = ((bf16[8,1,8,256]{3,2,1,0:T(8,128)(2,1)}), bf16[8,1,8,256]{3,2,1,0:T(8,128)(2,1)S(1)}, u32[]{:S(2)}, u32[]{:S(2)}) async-start(bf16[8,1,8,256]{3,2,1,0:T(8,128)(2,1)} %bitcast.26), calls=%async_computation.1 | async-start | bytes 65536 | tf_op jit(solution)/shard_map/all_to_all | solution.py:129
  39.2 45.7 %reduce-scatter.5.cloned.1.call-start = ((), (), s32[]{:S(2)}) async-start(), calls=%async_computation.13 | async-start | bytes 589824 | tf_op jit(solution)/shard_map/reduce_scatter | solution.py:211
  89.2 9.2 %all-to-all-start.2 = ((f32[8,1,2048]{2,1,0:T(1,128)}), f32[8,1,2048]{2,1,0:T(1,128)S(1)}, u32[]{:S(2)}, u32[]{:S(2)}) async-start(f32[8,1,2048]{2,1,0:T(1,128)} %reshape.880), calls=%async_computation.3 | async-start | bytes 131072 | tf_op jit(solution)/shard_map/all_to_all | solution.py:218
  92.6 33.5 %all-reduce.6.cloned.1.call-start = ((), (), s32[]{:S(2)}) async-start(), calls=%async_computation.14 | async-start | bytes 131072 | tf_op jit(solution)/shard_map/psum | solution.py:222
  105.8 0.7 copy-start.31
  133.2 10.6 %all-to-all-start.3 = ((f32[8,1,2048]{2,1,0:T(1,128)}), f32[8,1,2048]{2,1,0:T(1,128)}, u32[]{:S(2)}, u32[]{:S(2)}) async-start(f32[8,1,2048]{2,1,0:T(1,128)} %reshape.882), calls=%async_computation.4 | async-start | bytes 131072 | tf_op jit(solution)/shard_map/all_to_all | solution.py:179
  137.8 80.9 %reduce-scatter.7.cloned.1.call-start = ((), (), s32[]{:S(2)}) async-start(), calls=%async_computation.15 | async-start | bytes 589824 | tf_op jit(solution)/shard_map/reduce_scatter | solution.py:211
  169.7 1.6 copy-start.10
  171.3 0.7 copy-start.9
  172.8 1.6 copy-start.10
  174.5 0.7 copy-start.9
  176.0 1.6 copy-start.10
  177.7 0.7 copy-start.9
  179.2 1.6 copy-start.10
  189.7 61.7 %all-reduce.8.cloned.1.call-start = ((), (), s32[]{:S(2)}) async-start(), calls=%async_computation.16 | async-start | bytes 131072 | tf_op jit(solution)/shard_map/psum | solution.py:222
  251.5 1.4 copy-start.15
  252.5 1.0 copy-start.5
  252.9 1.1 copy-start.2
  258.9 10.6 %all-to-all-start.5 = ((f32[8,1,2048]{2,1,0:T(1,128)}), f32[8,1,2048]{2,1,0:T(1,128)}, u32[]{:S(2)}, u32[]{:S(2)}) async-start(f32[8,1,2048]{2,1,0:T(1,128)} %reshape.886), calls=%async_computation.7 | async-start | bytes 131072 | tf_op jit(solution)/shard_map/all_to_all | solution.py:179
  263.5 81.0 %reduce-scatter.9.cloned.1.call-start = ((), (), s32[]{:S(2)}) async-start(), calls=%async_computation.17 | async-start | bytes 589824 | tf_op jit(solution)/shard_map/reduce_scatter | solution.py:211
  295.3 1.6 copy-start.12
  296.9 0.7 copy-start.11
  298.5 1.6 copy-start.12
  301.6 1.6 copy-start.12
  304.8 1.6 copy-start.12
  315.4 61.6 %all-reduce.10.cloned.1.call-start = ((), (), s32[]{:S(2)}) async-start(), calls=%async_computation.18 | async-start | bytes 131072 | tf_op jit(solution)/shard_map/psum | solution.py:222
  377.0 1.4 copy-start.16
  378.0 1.0 copy-start.6
  378.4 1.1 copy-start.3
  384.4 10.6 %all-to-all-start.7 = ((f32[8,1,2048]{2,1,0:T(1,128)}), f32[8,1,2048]{2,1,0:T(1,128)}, u32[]{:S(2)}, u32[]{:S(2)}) async-start(f32[8,1,2048]{2,1,0:T(1,128)} %reshape.890), calls=%async_computation.10 | async-start | bytes 131072 | tf_op jit(solution)/shard_map/all_to_all | solution.py:179
  389.0 81.0 %reduce-scatter.11.cloned.1.call-start = ((), (), s32[]{:S(2)}) async-start(), calls=%async_computation.19 | async-start | bytes 589824 | tf_op jit(solution)/shard_map/reduce_scatter | solution.py:211
  419.3 0.7 copy-start.7
  420.9 1.6 copy-start.8
  422.5 0.7 copy-start.7
  424.0 1.6 copy-start.8
  425.7 0.7 copy-start.7
  427.2 1.6 copy-start.8
  428.9 0.7 copy-start.7
  430.4 1.6 copy-start.8
  441.0 61.5 %all-reduce.12.cloned.1.call-start = ((), (), s32[]{:S(2)}) async-start(), calls=%async_computation.20 | async-start | bytes 131072 | tf_op jit(solution)/shard_map/psum | solution.py:222
  (20 other events, 13.5 us)
Sparse Core Ops, SparseCore 0:
  55.3 29.5 reduce-scatter.4
  106.6 19.3 all-reduce.5
  189.9 28.8 reduce-scatter.6
  231.9 19.5 all-reduce.7
  315.5 28.9 reduce-scatter.8
  357.6 19.3 all-reduce.9
  441.1 28.8 reduce-scatter.10
  483.1 19.3 all-reduce.11
where the time goes:
time: 516 us; the launch traced here: 512 us
  waiting for transfers between devices  215 us (42%)
  blocking collectives  78.2 us (15%)
  local copies, waits for them, and re-layouts  69.4 us (13%)
  matrix products  62 us (12%)
  other arithmetic  46.1 us (9%)
  starting transfers between devices  26.2 us (5%)
  between operations  15.1 us (3%)
    reduce_scatter x4, waiting for transfers between devices, local(): lax.psum_scatter(grid_term(jnp.int32(0), row_count * lax.axis_size(('tile...  111 us
    psum x4, waiting for transfers between devices, local(): gradient = lax.psum(conj_mul(coil_sens, coil_back), 'coil')  77.4 us
    all_gather x3, blocking collectives, local(): piece = lax.all_gather(kspace, ('tile', 'spk'), axis=0, tiled=True)  42.6 us
    dot_general x16, matrix products, grid_one_spoke(): jnp.dot(smeared.reshape(piece_rows * 2, RO), row_one, preferred_element_t...  29.2 us
    all_to_all x3, blocking collectives, local(): lax.all_to_all(partial_back, ('tile', 'spk'), split_axis=2, concat_axis=0...  24.9 us
    unnamed x82, local copies, waits for them, and re-layouts  24.4 us
    all_to_all x3, waiting for transfers between devices, local(): lax.all_to_all(half_done, ('tile', 'spk'), split_axis=2, concat_axis=0, t...  17.1 us
    dynamic_update_slice x12, other arithmetic, fold_one_spoke(): lax.dynamic_update_index_in_dim(partial_value, current + added, spoke_ind...  15.1 us
  transfers between devices with their start and end apart: 14, of which 13 were waited for; matrix products, arithmetic and copies ran while one was open for 3% of the time, Pallas kernels for 0%

commit v1 on v0

--- a/solution.py
+++ b/solution.py
@@ -176,8 +176,14 @@
         else:
             coil_image = complex_mul(coil_sens, estimate)
             half_done = jnp.einsum("rpc,pcqv->rqv", coil_image, fwd_table, precision=HIGH)
-            turned = lax.all_to_all(
-                half_done, ("tile", "spk"), split_axis=2, concat_axis=0, tiled=True
+            turned = jnp.concatenate(
+                lax.all_to_all(
+                    jnp.stack(jnp.split(half_done, lax.axis_size(("tile", "spk")), axis=2)),
+                    ("tile", "spk"),
+                    0,
+                    0,
+                ),
+                axis=0,
             )
             kspace = jnp.einsum("rpv,prqu->vqu", turned, fwd_table, precision=HIGH).astype(
                 jnp.bfloat16

time: 516 us -> 511 us (level)
    all_to_all x6 -> x3, local copies, waits for them, and re-layouts: 10.5 us -> 5.35 us  [local(): lax.all_to_all(jnp.stack(jnp.split(half_done, lax.axis_size(('tile', 'spk...]
    unnamed x82 -> x112, local copies, waits for them, and re-layouts: 24.4 us -> 26.2 us
where the time goes in v1:
time: 511 us; the launch traced here: 508 us
  waiting for transfers between devices  215 us (42%)
  blocking collectives  78.4 us (15%)
  local copies, waits for them, and re-layouts  66.2 us (13%)
  matrix products  60.3 us (12%)
  other arithmetic  46 us (9%)
  starting transfers between devices  25.8 us (5%)
  between operations  15.2 us (3%)
    reduce_scatter x4, waiting for transfers between devices, local(): lax.psum_scatter(grid_term(jnp.int32(0), row_count * lax.axis_size(('tile...  112 us
    psum x4, waiting for transfers between devices, local(): gradient = lax.psum(conj_mul(coil_sens, coil_back), 'coil')  77.2 us
    all_gather x3, blocking collectives, local(): piece = lax.all_gather(kspace, ('tile', 'spk'), axis=0, tiled=True)  42.9 us
    dot_general x16, matrix products, grid_one_spoke(): jnp.dot(smeared.reshape(piece_rows * 2, RO), row_one, preferred_element_t...  29.3 us
    unnamed x112, local copies, waits for them, and re-layouts  26.2 us
    all_to_all x3, blocking collectives, local(): lax.all_to_all(partial_back, ('tile', 'spk'), split_axis=2, concat_axis=0...  24.9 us
    all_to_all x3, waiting for transfers between devices, local(): lax.all_to_all(jnp.stack(jnp.split(half_done, lax.axis_size(('tile', 'spk...  17.3 us
    dynamic_update_slice x12, other arithmetic, fold_one_spoke(): lax.dynamic_update_index_in_dim(partial_value, current + added, spoke_ind...  15.1 us
  transfers between devices with their start and end apart: 14, of which 13 were waited for; matrix products, arithmetic and copies ran while one was open for 3% of the time, Pallas kernels for 0%

profile of v1, /device:TPU:0, one launch (start us, length us, event | category | flops | bytes accessed | tf_op | source)
XLA Modules:
  0.0 507.7 jit_solution(15765767126400243369)
XLA Ops:
  8.6 10.6 %all-reduce = s32[8]{0:T(128)S(1)} all-reduce(s32[8]{0:T(128)S(1)} %dynamic-update-slice), channel_id=1, replica_groups=mesh['grp'=2,'tile'=4,'coil'=2,'spk'=2] {'tile','spk'}, use_global_device_ids=true, to_apply=%add | all-reduce | flops 8 | bytes 64
  22.0 3.3 all-to-all-start
  33.5 5.0 all-to-all-start.1
  39.2 5.1 %all-to-all-done.1 = bf16[8,1,8,256]{3,2,1,0:T(8,128)(2,1)S(1)} async-done(((bf16[8,1,8,256]{3,2,1,0:T(8,128)(2,1)}), bf16[8,1,8,256]{3,2,1,0:T(8,128)(2,1)S(1)}, u32[]{:S(2)}, u32[]{:S(2)}) %all-to-all-start.1) | async-done | bytes 32800 | tf_op jit(solution)/shard_map/all_to_all | solution.py:129
  47.0 7.6 %while.98 = (s32[]{:T(128)}, f32[256,2,256]{2,0,1:T(8,128)}, bf16[4,256,256]{2,1,0:T(8,128)(2,1)S(1)}, f32[4,2,256]{2,1,0:T(2,128)S(1)}, bf16[4,256,256]{2,1,0:T(8,128)(2,1)S(1)}, /*index=5*/s32[]{:T(128)}, s32[]{:T(128)}) while((s32[]{:T(128)}, f32[256,2,256]{2,0,1:T(8,128)}, bf16[4,256,256]{2,1,0:T(8,128)(2,1)S(1)}, ...), condition=%wide.region_3.4_spmd.clone, body=%wide.region_2.3_spmd.clone.sunk | while | flops 67698688 | bytes 1841251 | solution.py:166
  48.1 2.1 convolution_add_fusion.8
  50.3 2.1 convolution_add_fusion.8
  52.4 2.1 convolution_add_fusion.8
  56.4 2.6 select_select_fusion
  59.8 24.6 %reduce-scatter.5.cloned.1.call-done = f32[32,2,256]{2,0,1:T(8,128)} async-done(((f32[256,2,256]{2,0,1:T(8,128)}), f32[32,2,256]{2,0,1:T(8,128)}) %reduce-scatter.5.cloned.1.call-update) | async-done | bytes 65552 | tf_op jit(solution)/shard_map/reduce_scatter | solution.py:217
  88.7 3.4 all-to-all-start.2
  94.1 3.8 all-to-all-done.2
  106.8 18.6 %all-reduce.6.cloned.1.call-done = f32[32,2,256]{2,0,1:T(8,128)} async-done(((f32[32,2,256]{2,0,1:T(8,128)}), f32[32,2,256]{2,0,1:T(8,128)}) %all-reduce.6.cloned.1.call-update) | async-done | bytes 65552 | tf_op jit(solution)/shard_map/psum | solution.py:228
  131.4 4.6 all-to-all-start.3
  136.6 5.4 %all-to-all-done.3 = f32[8,1,2048]{2,1,0:T(1,128)} async-done(((f32[8,1,2048]{2,1,0:T(1,128)}), f32[8,1,2048]{2,1,0:T(1,128)}, u32[]{:S(2)}, u32[]{:S(2)}) %all-to-all-start.3) | async-done | bytes 65568 | tf_op jit(solution)/shard_map/all_to_all | solution.py:180
  142.0 2.3 reduce.1
  151.0 14.4 %all_gather.13 = bf16[256,2,256]{2,0,1:T(8,128)(2,1)S(1)} all-gather(bf16[32,2,256]{2,0,1:T(8,128)(2,1)S(1)} %fusion.32), channel_id=1, replica_groups=mesh['grp'=2,'tile'=4,'coil'=2,'spk'=2] {'tile','spk'}, dimensions={0}, use_global_device_ids=true | all-gather | bytes 294912 | tf_op jit(solution)/shard_map/all_gather | solution.py:191
  166.4 12.7 %while.95 = (s32[]{:T(128)}, f32[4,2,256]{2,1,0:T(2,128)}, bf16[4,256,256]{2,1,0:T(8,128)(2,1)S(1)}, bf16[512,256]{1,0:T(8,128)(2,1)S(1)}, bf16[4,256,256]{2,1,0:T(8,128)(2,1)S(1)}, /*index=5*/s32[]{:T(128)}) while((s32[]{:T(128)}, f32[4,2,256]{2,1,0:T(2,128)}, bf16[4,256,256]{2,1,0:T(8,128)(2,1)S(1)}, bf16[512,256]{1,0:T(8,128)(2,1)S(1)}, ...), condition=%wide.region_8.9_spmd, body=%wide.region_6.8_spmd.sunk | while | flops 67436544 | bytes 6300293 | solution.py:212
  180.4 7.5 %while.99 = (s32[]{:T(128)}, f32[256,2,256]{2,0,1:T(8,128)}, bf16[4,256,256]{2,1,0:T(8,128)(2,1)S(1)}, f32[4,2,256]{2,1,0:T(2,128)S(1)}, bf16[4,256,256]{2,1,0:T(8,128)(2,1)S(1)}, /*index=5*/s32[]{:T(128)}, s32[]{:T(128)}) while((s32[]{:T(128)}, f32[256,2,256]{2,0,1:T(8,128)}, bf16[4,256,256]{2,1,0:T(8,128)(2,1)S(1)}, ...), condition=%wide.region_10.11_spmd.clone, body=%wide.region_9.10_spmd.clone.sunk | while | flops 67698688 | bytes 1841251 | solution.py:166
  181.6 2.1 convolution_add_fusion.9
  183.7 2.1 convolution_add_fusion.9
  185.9 2.1 convolution_add_fusion.9
  188.0 29.0 %reduce-scatter.7.cloned.1.call-done = f32[32,2,256]{2,0,1:T(8,128)} async-done(((f32[256,2,256]{2,0,1:T(8,128)}), f32[32,2,256]{2,0,1:T(8,128)}) %reduce-scatter.7.cloned.1.call-update) | async-done | bytes 65552 | tf_op jit(solution)/shard_map/reduce_scatter | solution.py:217
  219.0 8.3 %all_to_all.97 = f32[8,1,2048]{2,1,0:T(1,128)S(1)} all-to-all(f32[8,1,2048]{2,1,0:T(1,128)S(1)} %reshape.896), channel_id=1, replica_groups=mesh['grp'=2,'tile'=4,'coil'=2,'spk'=2] {'tile','spk'}, dimensions={0} | all-to-all | bytes 131072 | tf_op jit(solution)/shard_map/all_to_all | solution.py:224
  230.1 19.5 %all-reduce.8.cloned.1.call-done = f32[32,2,256]{2,0,1:T(8,128)} async-done(((f32[32,2,256]{2,0,1:T(8,128)}), f32[32,2,256]{2,0,1:T(8,128)}) %all-reduce.8.cloned.1.call-update) | async-done | bytes 65552 | tf_op jit(solution)/shard_map/psum | solution.py:228
  255.8 4.6 all-to-all-start.5
  260.4 6.0 %all-to-all-done.5 = f32[8,1,2048]{2,1,0:T(1,128)} async-done(((f32[8,1,2048]{2,1,0:T(1,128)}), f32[8,1,2048]{2,1,0:T(1,128)}, u32[]{:S(2)}, u32[]{:S(2)}) %all-to-all-start.5) | async-done | bytes 65568 | tf_op jit(solution)/shard_map/all_to_all | solution.py:180
  266.4 2.3 reduce.3
  275.3 14.2 %all_gather.14 = bf16[256,2,256]{2,0,1:T(8,128)(2,1)S(1)} all-gather(bf16[32,2,256]{2,0,1:T(8,128)(2,1)S(1)} %fusion.33), channel_id=1, replica_groups=mesh['grp'=2,'tile'=4,'coil'=2,'spk'=2] {'tile','spk'}, dimensions={0}, use_global_device_ids=true | all-gather | bytes 294912 | tf_op jit(solution)/shard_map/all_gather | solution.py:191
  290.5 12.7 %while.96 = (s32[]{:T(128)}, f32[4,2,256]{2,1,0:T(2,128)}, bf16[4,256,256]{2,1,0:T(8,128)(2,1)S(1)}, bf16[512,256]{1,0:T(8,128)(2,1)S(1)}, bf16[4,256,256]{2,1,0:T(8,128)(2,1)S(1)}, /*index=5*/s32[]{:T(128)}) while((s32[]{:T(128)}, f32[4,2,256]{2,1,0:T(2,128)}, bf16[4,256,256]{2,1,0:T(8,128)(2,1)S(1)}, bf16[512,256]{1,0:T(8,128)(2,1)S(1)}, ...), condition=%wide.region_15.16_spmd, body=%wide.region_13.15_spmd.sunk | while | flops 67436544 | bytes 6300293 | solution.py:212
  304.6 7.5 %while.100 = (s32[]{:T(128)}, f32[256,2,256]{2,0,1:T(8,128)}, bf16[4,256,256]{2,1,0:T(8,128)(2,1)S(1)}, f32[4,2,256]{2,1,0:T(2,128)S(1)}, bf16[4,256,256]{2,1,0:T(8,128)(2,1)S(1)}, /*index=5*/s32[]{:T(128)}, s32[]{:T(128)}) while((s32[]{:T(128)}, f32[256,2,256]{2,0,1:T(8,128)}, bf16[4,256,256]{2,1,0:T(8,128)(2,1)S(1)}, ...), condition=%wide.region_17.18_spmd.clone, body=%wide.region_16.17_spmd.clone.sunk | while | flops 67698688 | bytes 1841251 | solution.py:166
  305.8 2.1 convolution_add_fusion.10
  307.9 2.1 convolution_add_fusion.10
  310.0 2.1 convolution_add_fusion.10
  312.2 28.9 %reduce-scatter.9.cloned.1.call-done = f32[32,2,256]{2,0,1:T(8,128)} async-done(((f32[256,2,256]{2,0,1:T(8,128)}), f32[32,2,256]{2,0,1:T(8,128)}) %reduce-scatter.9.cloned.1.call-update) | async-done | bytes 65552 | tf_op jit(solution)/shard_map/reduce_scatter | solution.py:217
  343.1 8.3 %all_to_all.98 = f32[8,1,2048]{2,1,0:T(1,128)S(1)} all-to-all(f32[8,1,2048]{2,1,0:T(1,128)S(1)} %reshape.900), channel_id=1, replica_groups=mesh['grp'=2,'tile'=4,'coil'=2,'spk'=2] {'tile','spk'}, dimensions={0} | all-to-all | bytes 131072 | tf_op jit(solution)/shard_map/all_to_all | solution.py:224
  354.2 19.5 %all-reduce.10.cloned.1.call-done = f32[32,2,256]{2,0,1:T(8,128)} async-done(((f32[32,2,256]{2,0,1:T(8,128)}), f32[32,2,256]{2,0,1:T(8,128)}) %all-reduce.10.cloned.1.call-update) | async-done | bytes 65552 | tf_op jit(solution)/shard_map/psum | solution.py:228
  379.9 4.6 all-to-all-start.7
  384.5 6.0 %all-to-all-done.7 = f32[8,1,2048]{2,1,0:T(1,128)} async-done(((f32[8,1,2048]{2,1,0:T(1,128)}), f32[8,1,2048]{2,1,0:T(1,128)}, u32[]{:S(2)}, u32[]{:S(2)}) %all-to-all-start.7) | async-done | bytes 65568 | tf_op jit(solution)/shard_map/all_to_all | solution.py:180
  390.5 2.3 reduce.5
  399.5 14.2 %all_gather.15 = bf16[256,2,256]{2,0,1:T(8,128)(2,1)S(1)} all-gather(bf16[32,2,256]{2,0,1:T(8,128)(2,1)S(1)} %fusion.34), channel_id=1, replica_groups=mesh['grp'=2,'tile'=4,'coil'=2,'spk'=2] {'tile','spk'}, dimensions={0}, use_global_device_ids=true | all-gather | bytes 294912 | tf_op jit(solution)/shard_map/all_gather | solution.py:191
  414.7 12.7 %while.97 = (s32[]{:T(128)}, f32[4,2,256]{2,1,0:T(2,128)}, bf16[4,256,256]{2,1,0:T(8,128)(2,1)S(1)}, bf16[512,256]{1,0:T(8,128)(2,1)S(1)}, bf16[4,256,256]{2,1,0:T(8,128)(2,1)S(1)}, /*index=5*/s32[]{:T(128)}) while((s32[]{:T(128)}, f32[4,2,256]{2,1,0:T(2,128)}, bf16[4,256,256]{2,1,0:T(8,128)(2,1)S(1)}, bf16[512,256]{1,0:T(8,128)(2,1)S(1)}, ...), condition=%wide.region_22.23_spmd, body=%wide.region_20.22_spmd.sunk | while | flops 67436544 | bytes 6300293 | solution.py:212
  428.8 7.5 %while.101 = (s32[]{:T(128)}, f32[256,2,256]{2,0,1:T(8,128)}, bf16[4,256,256]{2,1,0:T(8,128)(2,1)S(1)}, f32[4,2,256]{2,1,0:T(2,128)S(1)}, bf16[4,256,256]{2,1,0:T(8,128)(2,1)S(1)}, /*index=5*/s32[]{:T(128)}, s32[]{:T(128)}) while((s32[]{:T(128)}, f32[256,2,256]{2,0,1:T(8,128)}, bf16[4,256,256]{2,1,0:T(8,128)(2,1)S(1)}, ...), condition=%wide.region_24.25_spmd.clone, body=%wide.region_23.24_spmd.clone.sunk | while | flops 67698688 | bytes 1841251 | solution.py:166
  430.0 2.1 convolution_add_fusion.11
  434.2 2.1 convolution_add_fusion.11
  436.4 29.0 %reduce-scatter.11.cloned.1.call-done = f32[32,2,256]{2,0,1:T(8,128)} async-done(((f32[256,2,256]{2,0,1:T(8,128)}), f32[32,2,256]{2,0,1:T(8,128)}) %reduce-scatter.11.cloned.1.call-update) | async-done | bytes 65552 | tf_op jit(solution)/shard_map/reduce_scatter | solution.py:217
  467.3 8.3 %all_to_all.99 = f32[8,1,2048]{2,1,0:T(1,128)S(1)} all-to-all(f32[8,1,2048]{2,1,0:T(1,128)S(1)} %reshape.904), channel_id=1, replica_groups=mesh['grp'=2,'tile'=4,'coil'=2,'spk'=2] {'tile','spk'}, dimensions={0} | all-to-all | bytes 131072 | tf_op jit(solution)/shard_map/all_to_all | solution.py:224
  478.4 19.6 %all-reduce.12.cloned.1.call-done = f32[32,2,256]{2,0,1:T(8,128)} async-done(((f32[32,2,256]{2,0,1:T(8,128)}), f32[32,2,256]{2,0,1:T(8,128)}) %all-reduce.12.cloned.1.call-update) | async-done | bytes 65552 | tf_op jit(solution)/shard_map/psum | solution.py:228
  (435 shorter events, 140.5 us)
Async XLA Ops:
  6.5 14.3 %copy-start = (s32[8,256]{1,0:T(8,128)S(1)}, s32[8,256]{1,0:T(8,128)}, u32[]{:S(2)}) copy-start(s32[8,256]{1,0:T(8,128)} %param.23) | copy-start | bytes 24580
  22.0 11.5 %all-to-all-start = ((s32[8,1,256]{2,1,0:T(1,128)}), s32[8,1,256]{2,1,0:T(1,128)S(1)}, u32[]{:S(2)}, u32[]{:S(2)}) async-start(s32[8,1,256]{2,1,0:T(1,128)} %copy.109), calls=%async_computation | async-start | bytes 16384 | tf_op jit(solution)/shard_map/all_to_all | solution.py:132
  27.4 31.6 %copy-start.29 = (s32[8]{0:T(128)}, s32[8]{0:T(128)S(1)}, u32[]{:S(2)}) copy-start(s32[8]{0:T(128)S(1)} %get-tuple-element.881) | copy-start | bytes 100
  27.4 31.5 %copy-start.31 = (s32[8]{0:T(128)}, s32[8]{0:T(128)S(1)}, u32[]{:S(2)}) copy-start(s32[8]{0:T(128)S(1)} %get-tuple-element.882) | copy-start | bytes 100
  28.2 0.7 copy-start.22
  29.0 1.3 copy-start.26
  30.5 118.9 %copy-start.1 = (f32[1,256,2,256]{3,1,2,0:T(8,128)}, f32[1,256,2,256]{3,1,2,0:T(8,128)S(1)}, u32[]{:S(2)}) copy-start(f32[1,256,2,256]{3,1,2,0:T(8,128)S(1)} %get-tuple-element.830) | copy-start | bytes 1572868
  30.5 118.9 %copy-start.4 = (f32[1,256,2,256]{3,1,2,0:T(8,128)}, f32[1,256,2,256]{3,1,2,0:T(8,128)S(1)}, u32[]{:S(2)}) copy-start(f32[1,256,2,256]{3,1,2,0:T(8,128)S(1)} %get-tuple-element.833) | copy-start | bytes 1572868
  33.5 10.8 %all-to-all-start.1 = ((bf16[8,1,8,256]{3,2,1,0:T(8,128)(2,1)}), bf16[8,1,8,256]{3,2,1,0:T(8,128)(2,1)S(1)}, u32[]{:S(2)}, u32[]{:S(2)}) async-start(bf16[8,1,8,256]{3,2,1,0:T(8,128)(2,1)} %bitcast.26), calls=%async_computation.1 | async-start | bytes 65536 | tf_op jit(solution)/shard_map/all_to_all | solution.py:129
  38.5 45.9 %reduce-scatter.5.cloned.1.call-start = ((), (), s32[]{:S(2)}) async-start(), calls=%async_computation.13 | async-start | bytes 589824 | tf_op jit(solution)/shard_map/reduce_scatter | solution.py:217
  88.7 9.2 %all-to-all-start.2 = ((f32[8,1,2048]{2,1,0:T(1,128)}), f32[8,1,2048]{2,1,0:T(1,128)S(1)}, u32[]{:S(2)}, u32[]{:S(2)}) async-start(f32[8,1,2048]{2,1,0:T(1,128)} %reshape.892), calls=%async_computation.3 | async-start | bytes 131072 | tf_op jit(solution)/shard_map/all_to_all | solution.py:224
  92.0 33.4 %all-reduce.6.cloned.1.call-start = ((), (), s32[]{:S(2)}) async-start(), calls=%async_computation.14 | async-start | bytes 131072 | tf_op jit(solution)/shard_map/psum | solution.py:228
  105.2 0.7 copy-start.34
  128.9 0.7 copy-start.13
  131.4 10.6 %all-to-all-start.3 = ((f32[8,1,2048]{2,1,0:T(1,128)}), f32[8,1,2048]{2,1,0:T(1,128)}, u32[]{:S(2)}, u32[]{:S(2)}) async-start(f32[8,1,2048]{2,1,0:T(1,128)} %reshape.894), calls=%async_computation.4 | async-start | bytes 131072 | tf_op jit(solution)/shard_map/all_to_all | solution.py:180
  136.0 81.0 %reduce-scatter.7.cloned.1.call-start = ((), (), s32[]{:S(2)}) async-start(), calls=%async_computation.15 | async-start | bytes 589824 | tf_op jit(solution)/shard_map/reduce_scatter | solution.py:217
  167.9 1.6 copy-start.10
  171.1 1.6 copy-start.10
  174.2 1.6 copy-start.10
  177.4 1.6 copy-start.10
  188.0 61.6 %all-reduce.8.cloned.1.call-start = ((), (), s32[]{:S(2)}) async-start(), calls=%async_computation.16 | async-start | bytes 131072 | tf_op jit(solution)/shard_map/psum | solution.py:228
  249.6 1.4 copy-start.18
  250.6 1.0 copy-start.5
  251.0 1.1 copy-start.2
  253.3 0.7 copy-start.14
  255.8 10.6 %all-to-all-start.5 = ((f32[8,1,2048]{2,1,0:T(1,128)}), f32[8,1,2048]{2,1,0:T(1,128)}, u32[]{:S(2)}, u32[]{:S(2)}) async-start(f32[8,1,2048]{2,1,0:T(1,128)} %reshape.898), calls=%async_computation.7 | async-start | bytes 131072 | tf_op jit(solution)/shard_map/all_to_all | solution.py:180
  260.4 80.8 %reduce-scatter.9.cloned.1.call-start = ((), (), s32[]{:S(2)}) async-start(), calls=%async_computation.17 | async-start | bytes 589824 | tf_op jit(solution)/shard_map/reduce_scatter | solution.py:217
  292.1 1.6 copy-start.12
  295.2 1.6 copy-start.12
  298.4 1.6 copy-start.12
  300.0 0.7 copy-start.11
  301.6 1.6 copy-start.12
  312.2 61.5 %all-reduce.10.cloned.1.call-start = ((), (), s32[]{:S(2)}) async-start(), calls=%async_computation.18 | async-start | bytes 131072 | tf_op jit(solution)/shard_map/psum | solution.py:228
  373.7 1.4 copy-start.19
  374.8 1.0 copy-start.6
  375.1 1.1 copy-start.3
  377.4 0.7 copy-start.15
  379.9 10.6 %all-to-all-start.7 = ((f32[8,1,2048]{2,1,0:T(1,128)}), f32[8,1,2048]{2,1,0:T(1,128)}, u32[]{:S(2)}, u32[]{:S(2)}) async-start(f32[8,1,2048]{2,1,0:T(1,128)} %reshape.902), calls=%async_computation.10 | async-start | bytes 131072 | tf_op jit(solution)/shard_map/all_to_all | solution.py:180
  384.5 80.9 %reduce-scatter.11.cloned.1.call-start = ((), (), s32[]{:S(2)}) async-start(), calls=%async_computation.19 | async-start | bytes 589824 | tf_op jit(solution)/shard_map/reduce_scatter | solution.py:217
  414.7 0.7 copy-start.7
  416.2 1.6 copy-start.8
  417.9 0.7 copy-start.7
  419.4 1.6 copy-start.8
  421.1 0.7 copy-start.7
  422.6 1.6 copy-start.8
  424.2 0.7 copy-start.7
  425.8 1.6 copy-start.8
  436.3 61.6 %all-reduce.12.cloned.1.call-start = ((), (), s32[]{:S(2)}) async-start(), calls=%async_computation.20 | async-start | bytes 131072 | tf_op jit(solution)/shard_map/psum | solution.py:228
  (23 other events, 15.5 us)
Sparse Core Ops, SparseCore 0:
  54.7 29.6 reduce-scatter.4
  106.0 19.3 all-reduce.5
  188.1 28.8 reduce-scatter.6
  230.2 19.3 all-reduce.7
  312.3 28.8 reduce-scatter.8
  354.3 19.3 all-reduce.9
  436.4 28.8 reduce-scatter.10
  478.5 19.3 all-reduce.11
